TPU v7x, 32 devices: a whole 2x2x4 slice. The times are simulated.
32 devices in a mesh: band: 16 (over z, y, core), fft: 2 (over x).
Axes of the slice: x: 2, y: 2, z: 4, core: 2. Of those that a mesh axis runs over, the one named last changes fastest.
Arguments:
- coefficients: float32 [16, 2, 72, 5184], P('band', None, None, 'fft'), may hold values from -0.009765625 to 0.009765625
- col_index: int32 [5184], replicated, may hold values from 0 to 5183, each once
- occupation: int32 [16], P('band'), may hold values from 1 to 4
Outputs:
- density: float32 [288, 288, 288], P('band', 'fft')
Inputs may be any that keep to these rules, and one draw needn't show every extreme that they name: `col_index`: each number of the range appears once.
All inputs are finite; a program needn't handle non-finite values.
Results may differ from a plain program's by a relative error of at most 0.0003.
Values sent between devices are 32-bit elements; how exact they have to be, the bound alone decides.
A program may use at most 128 MiB of HBM per device.

v0:
```python
import math
import jax
import jax.numpy as jnp
from jax import lax
from jax.sharding import PartitionSpec as P

NC = 144
NF = 288
KZ = 72
NCOLS = 5184


def product(pattern, operand_a, operand_b):
    return jnp.einsum(pattern, operand_a, operand_b, precision=lax.Precision.HIGHEST)


def phase_tables(wave_count, offset, points):
    wave_index = jnp.arange(wave_count, dtype=jnp.int32) - offset
    grid_index = jnp.arange(points, dtype=jnp.int32)
    phases = jnp.mod(wave_index[:, None] * grid_index[None, :], points)
    angles = phases.astype(jnp.float32) * (2.0 * math.pi / points)
    return (jnp.cos(angles), jnp.sin(angles))


def interpolation_matrix(coarse_len, fine_len):
    fine_index = jnp.arange(fine_len, dtype=jnp.int32)
    coarse_index = jnp.arange(coarse_len, dtype=jnp.int32)
    wave_index = jnp.arange(1, coarse_len // 2, dtype=jnp.int32)
    offsets = fine_index[:, None] - 2 * coarse_index[None, :]
    phases = jnp.mod(offsets[:, :, None] * wave_index[None, None, :], fine_len)
    angles = phases.astype(jnp.float32) * (2.0 * math.pi / fine_len)
    return (1.0 + 2.0 * jnp.sum(jnp.cos(angles), axis=2)) / coarse_len


def rotate(pattern, real_part, imag_part, cos_table, sin_table):
    out_real = product(pattern, real_part, cos_table) - product(pattern, imag_part, sin_table)
    out_imag = product(pattern, real_part, sin_table) + product(pattern, imag_part, cos_table)
    return (out_real, out_imag)


def local(coefficients, col_index, occupation):
    band_here = coefficients.shape[0]
    col_count = coefficients.shape[3]
    band_total = band_here * lax.axis_size("band")
    radius = KZ // 2
    col_start = lax.axis_index("fft") * col_count
    local_cols = lax.dynamic_slice_in_dim(col_index, col_start, col_count)
    first_wave = local_cols // KZ - radius
    second_wave = local_cols % KZ - radius
    third_wave = jnp.arange(KZ, dtype=jnp.int32) - radius
    radial = (first_wave * first_wave + second_wave * second_wave)[None, :] + (
        third_wave * third_wave
    )[:, None]
    inside = (radial <= radius * radius).astype(jnp.float32)
    masked = coefficients * inside
    cos_table, sin_table = phase_tables(KZ, radius, NC)
    line_real, line_imag = rotate("bkc,kz->bzc", masked[:, 0], masked[:, 1], cos_table, sin_table)
    z_lines = jnp.stack([line_real, line_imag], axis=1)
    inverse = jnp.zeros((NCOLS,), jnp.int32).at[col_index].set(jnp.arange(NCOLS, dtype=jnp.int32))
    block_in = lax.all_to_all(z_lines, "fft", split_axis=2, concat_axis=3, tiled=True)
    box_grid = jnp.take(block_in, inverse, axis=3)
    box_grid = box_grid.reshape(block_in.shape[0], 2, block_in.shape[2], KZ, KZ)
    half_real, half_imag = rotate(
        "bzak,kr->bzar", box_grid[:, 0], box_grid[:, 1], cos_table, sin_table
    )
    full_real, full_imag = rotate("bzar,as->bzsr", half_real, half_imag, cos_table, sin_table)
    moduli = full_real * full_real + full_imag * full_imag
    weights = occupation.astype(jnp.float32) / band_total
    partial_value = product("b,bzxy->zxy", weights, moduli)
    interpolation = interpolation_matrix(NC, NF)
    row_share = NF // lax.axis_size("band")
    summed = lax.psum(partial_value, "band")
    own_rows = lax.dynamic_slice_in_dim(
        interpolation, lax.axis_index("band") * row_share, row_share, 0
    )
    reduced = product("zgb,fb->zgf", product("zab,ga->zgb", summed, own_rows), interpolation)
    return product(
        "rgf,hr->gfh",
        lax.all_to_all(reduced, "fft", split_axis=2, concat_axis=0, tiled=True),
        interpolation,
    )


def solution(mesh):
    return jax.shard_map(
        local,
        mesh=mesh,
        in_specs=(P("band", None, None, "fft"), P(), P("band")),
        out_specs=P("band", "fft", None),
        check_vma=False,
    )
```

profile of v0, /device:TPU:0, one launch (start us, length us, event | category | flops | bytes accessed | tf_op | source)
XLA Modules:
  0.0 451.8 jit_solution(9786847167849780601)
XLA Ops:
  7.5 1.6 broadcast_multiply_fusion
  9.1 1.6 fusion.18
  10.7 1.6 fusion.19
  12.4 1.7 fusion.8
  14.1 1.7 fusion.7
  16.0 3.2 copy.44
  19.3 4.2 all-to-all-start
  23.5 36.3 %scatter_custom_fusion = s32[5184]{0:T(1024)S(1)} fusion(s32[5184]{0:T(1024)S(1)} %compare_select_fusion.1, s32[5184]{0:T(1024)S(1)} %iota.59, s32[]{:T(128)} %constant.53.clone.1), kind=kCustom, calls=%fused_computation.112 | custom fusion | bytes 20740 | tf_op jit(solution)/shard_map/scatter | solution.py:59
  60.6 6.9 %copy.62 = f32[1,2,72,2,2592]{2,1,4,3,0:T(2,128)} copy(f32[1,2,72,2,2592]{4,1,2,3,0:T(2,128)S(1)} %bitcast.89) | data formatting | bytes 5971968 | tf_op jit(solution)/shard_map/all_to_all | solution.py:60
  67.5 19.1 %gather_fusion = f32[5184,2,72]{2,1,0:T(2,128)} fusion(f32[2,72,5184]{1,0,2:T(2,128)} %bitcast.87, s32[6144]{0:T(1024)S(1)} %pad_clamp_fusion), kind=kCustom, calls=%fused_computation | custom fusion | bytes 5992704 | tf_op jit(solution)/shard_map/jit(_take)/gather | solution.py:61
  86.6 8.5 %copy.63 = f32[1,2,72,72,72]{4,3,2,1,0:T(8,128)} copy(f32[1,2,72,72,72]{2,1,4,3,0:T(2,128)} %bitcast.88) | data formatting | bytes 5971968 | tf_op jit(solution)/shard_map/jit(_take)/gather | solution.py:61
  95.0 2.9 broadcast_select_fusion
  97.9 4.8 %fusion.10 = f32[72,72,144]{2,1,0:T(8,128)S(1)} fusion(f32[1,2,72,72,72]{4,3,2,1,0:T(8,128)S(1)} %broadcast_select_fusion, s32[72]{0:T(128)S(1)} %iota_add_fusion), kind=kOutput, calls=%fused_computation.22 | convolution fusion | flops 645065856 | bytes 5640704 | tf_op jit(solution)/shard_map/bzak,kr->bzar/dot_general | solution.py:14
  102.7 4.8 %fusion.13 = f32[72,72,144]{2,1,0:T(8,128)S(1)} fusion(f32[72,72,144]{2,1,0:T(8,128)S(1)} %fusion.10, f32[1,2,72,72,72]{4,3,2,1,0:T(8,128)S(1)} %broadcast_select_fusion, s32[72]{0:T(128)S(1)} %iota_add_fusion), kind=kOutput, calls=%fused_computation.25 | convolution fusion | flops 645812352 | bytes 10949120 | tf_op jit(solution)/shard_map/bzak,kr->bzar/dot_general | solution.py:14
  107.5 11.8 %fusion.26 = f32[144,72,144]{2,0,1:T(8,128)} fusion(f32[72,72,144]{2,1,0:T(8,128)S(1)} %fusion.13, s32[72]{0:T(128)S(1)} %iota_add_fusion), kind=kOutput, calls=%fused_computation.46 | convolution fusion | flops 1290038400 | bytes 8958240 | tf_op jit(solution)/shard_map/bzar,as->bzsr/dot_general | solution.py:14
  119.3 12.0 %fusion.34 = f32[144,72,144]{2,0,1:T(8,128)} fusion(f32[72,72,144]{2,1,0:T(8,128)S(1)} %fusion.13, s32[72]{0:T(128)S(1)} %iota_add_fusion), kind=kOutput, calls=%fused_computation.54 | convolution fusion | flops 1290038400 | bytes 8958240 | tf_op jit(solution)/shard_map/bzar,as->bzsr/dot_general | solution.py:14
  131.3 4.8 %fusion.9 = f32[72,72,144]{2,1,0:T(8,128)S(1)} fusion(f32[1,2,72,72,72]{4,3,2,1,0:T(8,128)S(1)} %broadcast_select_fusion, s32[72]{0:T(128)S(1)} %iota_add_fusion), kind=kOutput, calls=%fused_computation.21 | convolution fusion | flops 645065856 | bytes 5640704 | tf_op jit(solution)/shard_map/bzak,kr->bzar/dot_general | solution.py:14
  136.1 4.8 %fusion.14 = f32[72,72,144]{2,1,0:T(8,128)S(1)} fusion(f32[72,72,144]{2,1,0:T(8,128)S(1)} %fusion.9, f32[1,2,72,72,72]{4,3,2,1,0:T(8,128)S(1)} %broadcast_select_fusion, s32[72]{0:T(128)S(1)} %iota_add_fusion), kind=kOutput, calls=%fused_computation.26 | convolution fusion | flops 645812352 | bytes 10949120 | tf_op jit(solution)/shard_map/bzak,kr->bzar/dot_general | solution.py:14
  140.9 11.7 %fusion.28 = f32[144,72,144]{2,0,1:T(8,128)} fusion(f32[72,72,144]{2,1,0:T(8,128)S(1)} %fusion.14, s32[72]{0:T(128)S(1)} %iota_add_fusion), kind=kOutput, calls=%fused_computation.48 | convolution fusion | flops 1290038400 | bytes 8958240 | tf_op jit(solution)/shard_map/bzar,as->bzsr/dot_general | solution.py:14
  152.6 21.9 %multiply_bitcast_fusion = f32[72,144,144]{2,1,0:T(8,128)} fusion(f32[144,72,144]{2,0,1:T(8,128)} %fusion.26, f32[144,72,144]{2,0,1:T(8,128)} %fusion.34, f32[144,72,144]{2,0,1:T(8,128)} %fusion.28, f32[]{:T(128)} %bitcast.1, f32[72,72,144]{2,1,0:T(8,128)} %copy-done, s32[72]{0:T(128)S(1)} %iota_add_fusion), kind=kOutput, calls=%fused_computation.11 | convolution fusion | flops 1298996352 | bytes 26874148 | tf_op jit(solution)/shard_map/bzar,as->bzsr/dot_general | solution.py:14
  174.6 61.2 %fusion.3 = f32[288,144]{0,1:T(8,128)S(1)} fusion(s32[71]{0:T(128)S(1)} %iota_add_fusion.1, s32[288,144]{0,1:T(8,128)S(1)} %iota_subtract_fusion), kind=kLoop, calls=%fused_computation.6 | loop fusion | flops 29403648 | bytes 332060 | tf_op jit(solution)/shard_map/reduce_sum | solution.py:32
  235.9 144.0 %all-reduce.2.cloned.1.call-done = f32[72,144,144]{2,1,0:T(8,128)} async-done(((f32[72,144,144]{2,1,0:T(8,128)}), f32[72,144,144]{2,1,0:T(8,128)}) %all-reduce.2.cloned.1.call-update) | async-done | bytes 5971984 | tf_op jit(solution)/shard_map/psum | solution.py:72
  379.9 8.3 %convolution_bitcast_fusion = f32[72,18,144]{2,1,0:T(8,128)S(1)} fusion(f32[72,144,144]{2,1,0:T(8,128)} %all-reduce.2.cloned.1.call-done, f32[288,144]{0,1:T(8,128)S(1)} %add_multiply_fusion, s32[]{:T(128)S(6)} %select_n.74), kind=kOutput, calls=%fused_computation.27 | convolution fusion | flops 322486272 | bytes 6792196 | tf_op jit(solution)/shard_map/zab,ga->zgb/dot_general | solution.py:14
  388.2 3.8 fusion.15
  392.0 3.5 copy.54
  395.5 3.8 reshape.191
  399.2 22.0 %all_to_all.36 = f32[2,1,186624]{2,1,0:T(1,128)S(1)} all-to-all(f32[2,1,186624]{2,1,0:T(1,128)} %reshape.191), channel_id=1, replica_groups=mesh['band'=16,'fft'=2] {'fft'}, dimensions={0} | all-to-all | bytes 2985984 | tf_op jit(solution)/shard_map/all_to_all | solution.py:79
  421.8 6.2 %reduce = f32[2,186624]{1,0:T(2,128)} reduce(f32[2,1,186624]{2,1,0:T(1,128)S(1)} %all_to_all.36, f32[]{:T(128)} %broadcast.120), dimensions={1}, to_apply=%all_to_all.30.reduce_sub_computation | reduce | bytes 2985988 | tf_op jit(solution)/shard_map/all_to_all | solution.py:79
  428.0 4.1 reshape.192
  432.1 3.6 copy.72
  435.7 3.3 all_to_all.33
  439.0 5.8 %fusion.20 = f32[18,144,288]{2,1,0:T(8,128)} fusion(f32[144,18,144]{0,2,1:T(8,128)S(1)} %all_to_all.33, f32[288,144]{0,1:T(8,128)S(1)} %copy-done.2), kind=kOutput, calls=%fused_computation.37 | convolution fusion | flops 1290069504 | bytes 4644864 | tf_op jit(solution)/shard_map/rgf,hr->gfh/dot_general | solution.py:14
  (27 shorter events, 2.1 us)
Async XLA Ops:
  16.0 7.5 %copy-start.3 = (s32[5184]{0:T(1024)S(1)}, s32[5184]{0:T(1024)}, u32[]{:S(2)}) copy-start(s32[5184]{0:T(1024)} %param.4) | copy-start | bytes 62212
  19.3 41.3 %all-to-all-start = ((f32[1,2,144,2592]{3,1,0,2:T(2,128)}), f32[1,2,144,2592]{3,1,0,2:T(2,128)S(1)}, u32[]{:S(2)}, u32[]{:S(2)}) async-start(f32[1,2,144,2592]{3,1,0,2:T(2,128)} %copy.44), calls=%async_computation | async-start | bytes 6193152 | tf_op jit(solution)/shard_map/all_to_all | solution.py:60
  23.5 356.4 %all-reduce.2.cloned.1.call-start = ((), (), s32[]{:S(2)}) async-start(), calls=%async_computation.2 | async-start | bytes 21233664 | tf_op jit(solution)/shard_map/psum | solution.py:72
  140.9 11.7 %copy-start = (f32[72,72,144]{2,1,0:T(8,128)}, f32[72,72,144]{2,1,0:T(8,128)S(1)}, u32[]{:S(2)}) copy-start(f32[72,72,144]{2,1,0:T(8,128)S(1)} %fusion.14) | copy-start | bytes 8957956
  235.8 152.3 %copy-start.1 = (f32[288,144]{0,1:T(8,128)}, f32[288,144]{0,1:T(8,128)S(1)}, u32[]{:S(2)}) copy-start(f32[288,144]{0,1:T(8,128)S(1)} %fusion.3) | copy-start | bytes 497668
  435.7 3.3 copy-start.2
Sparse Core Ops, SparseCore 0:
  174.6 205.2 all-reduce.1
where the time goes:
time: 460 us; the launch traced here: 452 us
  waiting for transfers between devices  144 us (31%)
  matrix products  101 us (22%)
  local copies, waits for them, and re-layouts  92.8 us (20%)
  other arithmetic  73.2 us (16%)
  blocking collectives  22 us (5%)
  between operations  14.5 us (3%)
    psum x1, waiting for transfers between devices, local(): summed = lax.psum(partial_value, 'band')  144 us
    dot_general x15, matrix products, product(): jnp.einsum(pattern, operand_a, operand_b, precision=lax.Precision.HIGHEST)  101 us
    reduce_sum x1, other arithmetic, interpolation_matrix(): return (1.0 + 2.0 * jnp.sum(jnp.cos(angles), axis=2)) / coarse_len  61.2 us
    scatter x1, local copies, waits for them, and re-layouts, local(): jnp.zeros((NCOLS,), jnp.int32).at[col_index]  36.3 us
    gather x2, local copies, waits for them, and re-layouts, local(): box_grid = jnp.take(block_in, inverse, axis=3)  27.5 us
    all_to_all x1, blocking collectives, local(): lax.all_to_all(reduced, 'fft', split_axis=2, concat_axis=0, tiled=True)  22 us
  transfers between devices with their start and end apart: 2, of which 1 were waited for; matrix products, arithmetic and copies ran while one was open for 22% of the time, Pallas kernels for 0%

commit v1 on v0

--- a/solution.py
+++ b/solution.py
@@ -69,7 +69,9 @@
     partial_value = product("b,bzxy->zxy", weights, moduli)
     interpolation = interpolation_matrix(NC, NF)
     row_share = NF // lax.axis_size("band")
-    summed = lax.psum(partial_value, "band")
+    summed = partial_value
+    for hop in (1, 2, 4, 8):
+        summed = summed + lax.ppermute(summed, "band", [(dev, dev ^ hop) for dev in range(16)])
     own_rows = lax.dynamic_slice_in_dim(
         interpolation, lax.axis_index("band") * row_share, row_share, 0
     )

time: 460 us -> 1190 us (2.59)
  waiting for transfers between devices: 144 us -> 867 us
  between operations: 14.5 us -> 1.11 us
    ppermute x0 -> x4, waiting for transfers between devices: none -> 867 us  [local(): lax.ppermute(summed, 'band', [(dev, dev ^ hop) for dev in range(16)])]
    psum x1 -> x0, waiting for transfers between devices: 144 us -> none  [local(): summed = lax.psum(partial_value, 'band')]
  transfers between devices with their start and end apart: 2 -> 5, of which waited for: 1 -> 4; matrix products, arithmetic and copies ran while one was open for 22% -> 8% of each run, Pallas kernels for 0% -> 0%
where the time goes in v1:
time: 1190 us; the launch traced here: 1180 us
  waiting for transfers between devices  867 us (73%)
  matrix products  103 us (9%)
  local copies, waits for them, and re-layouts  92.8 us (8%)
  other arithmetic  84.4 us (7%)
  blocking collectives  22 us (2%)
    ppermute x4, waiting for transfers between devices, local(): lax.ppermute(summed, 'band', [(dev, dev ^ hop) for dev in range(16)])  867 us
    dot_general x15, matrix products, product(): jnp.einsum(pattern, operand_a, operand_b, precision=lax.Precision.HIGHEST)  103 us
    reduce_sum x1, other arithmetic, interpolation_matrix(): return (1.0 + 2.0 * jnp.sum(jnp.cos(angles), axis=2)) / coarse_len  61 us
    scatter x1, local copies, waits for them, and re-layouts, local(): jnp.zeros((NCOLS,), jnp.int32).at[col_index]  36.3 us
    gather x2, local copies, waits for them, and re-layouts, local(): box_grid = jnp.take(block_in, inverse, axis=3)  27.5 us
  transfers between devices with their start and end apart: 5, of which 4 were waited for; matrix products, arithmetic and copies ran while one was open for 8% of the time, Pallas kernels for 0%

profile of v1, /device:TPU:0, one launch (start us, length us, event | category | flops | bytes accessed | tf_op | source)
XLA Modules:
  0.0 1181.3 jit_solution(17955237219741524194)
XLA Ops:
  9.5 3.2 copy.44
  12.8 4.2 all-to-all-start
  17.0 36.3 %scatter_custom_fusion = s32[5184]{0:T(1024)S(1)} fusion(s32[5184]{0:T(1024)S(1)} %compare_select_fusion.1, s32[5184]{0:T(1024)S(1)} %iota.59, s32[]{:T(128)} %constant.53.clone.1), kind=kCustom, calls=%fused_computation.114 | custom fusion | bytes 20740 | tf_op jit(solution)/shard_map/scatter | solution.py:59
  54.1 7.0 copy.62
  61.1 19.1 %gather_fusion = f32[5184,2,72]{2,1,0:T(2,128)} fusion(f32[2,72,5184]{1,0,2:T(2,128)} %bitcast.86, s32[6144]{0:T(1024)S(1)} %pad_clamp_fusion), kind=kCustom, calls=%fused_computation | custom fusion | bytes 5992704 | tf_op jit(solution)/shard_map/jit(_take)/gather | solution.py:61
  80.1 8.5 copy.63
  88.6 2.9 broadcast_select_fusion
  91.5 4.8 fusion.12
  96.3 4.8 fusion.15
  101.1 11.8 fusion.31
  112.9 12.0 %fusion.39 = f32[144,72,144]{2,0,1:T(8,128)} fusion(f32[72,72,144]{2,1,0:T(8,128)S(1)} %fusion.15, s32[72]{0:T(128)S(1)} %iota_add_fusion), kind=kOutput, calls=%fused_computation.56 | convolution fusion | flops 1290038400 | bytes 8958240 | tf_op jit(solution)/shard_map/bzar,as->bzsr/dot_general | solution.py:14
  124.9 4.8 fusion.11
  129.7 4.8 fusion.16
  134.5 11.7 fusion.33
  146.2 21.5 %multiply_bitcast_fusion = f32[72,144,144]{2,1,0:T(8,128)} fusion(f32[144,72,144]{2,0,1:T(8,128)} %fusion.31, f32[144,72,144]{2,0,1:T(8,128)} %fusion.39, f32[144,72,144]{2,0,1:T(8,128)} %fusion.33, f32[]{:T(128)} %bitcast.1, f32[72,72,144]{2,1,0:T(8,128)} %copy-done, s32[72]{0:T(128)S(1)} %iota_add_fusion), kind=kOutput, calls=%fused_computation.11 | convolution fusion | flops 1298996352 | bytes 26874148 | tf_op jit(solution)/shard_map/bzar,as->bzsr/dot_general | solution.py:14
  167.9 16.3 %collective-permute-done = f32[72,144,144]{2,1,0:T(8,128)S(1)} collective-permute-done((f32[72,144,144]{2,1,0:T(8,128)}, f32[72,144,144]{2,1,0:T(8,128)S(1)}, u32[]{:S(2)}, u32[]{:S(2)}) %collective-permute-start) | collective-permute-done | bytes 5972000 | tf_op jit(solution)/shard_map/ppermute | solution.py:74
  184.3 5.1 add.158
  192.2 228.5 %collective-permute-done.1 = f32[72,144,144]{2,1,0:T(8,128)S(1)} collective-permute-done((f32[72,144,144]{2,1,0:T(8,128)S(1)}, f32[72,144,144]{2,1,0:T(8,128)S(1)}, u32[]{:S(2)}, u32[]{:S(2)}) %collective-permute-start.1) | collective-permute-done | bytes 5972000 | tf_op jit(solution)/shard_map/ppermute | solution.py:74
  424.0 227.9 %collective-permute-done.2 = f32[72,144,144]{2,1,0:T(8,128)S(1)} collective-permute-done((f32[72,144,144]{2,1,0:T(8,128)S(1)}, f32[72,144,144]{2,1,0:T(8,128)S(1)}, u32[]{:S(2)}, u32[]{:S(2)}) %collective-permute-start.2) | collective-permute-done | bytes 5972000 | tf_op jit(solution)/shard_map/ppermute | solution.py:74
  651.8 4.9 add.160
  659.4 61.0 %fusion.3 = f32[288,144]{0,1:T(8,128)S(1)} fusion(s32[71]{0:T(128)S(1)} %iota_add_fusion.1, s32[288,144]{0,1:T(8,128)S(1)} %iota_subtract_fusion), kind=kLoop, calls=%fused_computation.6 | loop fusion | flops 29403648 | bytes 332060 | tf_op jit(solution)/shard_map/reduce_sum | solution.py:32
  720.5 393.8 %collective-permute-done.3 = f32[72,144,144]{2,1,0:T(8,128)} collective-permute-done((f32[72,144,144]{2,1,0:T(8,128)}, f32[72,144,144]{2,1,0:T(8,128)}, u32[]{:S(2)}, u32[]{:S(2)}) %collective-permute-start.3) | collective-permute-done | bytes 5972000 | tf_op jit(solution)/shard_map/ppermute | solution.py:74
  1114.3 10.2 fusion.17
  1124.5 3.8 fusion.20
  1128.3 3.5 copy.54
  1131.8 3.8 reshape.191
  1135.6 22.0 %all_to_all.36 = f32[2,1,186624]{2,1,0:T(1,128)S(1)} all-to-all(f32[2,1,186624]{2,1,0:T(1,128)} %reshape.191), channel_id=1, replica_groups=mesh['band'=16,'fft'=2] {'fft'}, dimensions={0} | all-to-all | bytes 2985984 | tf_op jit(solution)/shard_map/all_to_all | solution.py:81
  1158.2 6.2 reduce
  1164.3 4.1 reshape.192
  1168.4 3.6 copy.72
  1172.0 3.3 all_to_all.33
  1175.3 5.8 fusion.25
  (35 shorter events, 19.1 us)
Async XLA Ops:
  9.5 7.5 copy-start.3
  12.8 41.4 %all-to-all-start = ((f32[1,2,144,2592]{3,1,0,2:T(2,128)}), f32[1,2,144,2592]{3,1,0,2:T(2,128)S(1)}, u32[]{:S(2)}, u32[]{:S(2)}) async-start(f32[1,2,144,2592]{3,1,0,2:T(2,128)} %copy.44), calls=%async_computation | async-start | bytes 6193152 | tf_op jit(solution)/shard_map/all_to_all | solution.py:60
  134.5 11.7 copy-start
  167.7 16.6 %collective-permute-start = (f32[72,144,144]{2,1,0:T(8,128)}, f32[72,144,144]{2,1,0:T(8,128)S(1)}, u32[]{:S(2)}, u32[]{:S(2)}) collective-permute-start(f32[72,144,144]{2,1,0:T(8,128)} %multiply_bitcast_fusion), channel_id=1, source_target_pairs={{0,2},{2,0},{4,6},{6,4},{8,10},{10,8},{12,14},{14,12},{16,18},{18,... | collective-permute-start | bytes 17915912 | tf_op jit(solution)/shard_map/ppermute | solution.py:74
  189.4 231.3 %collective-permute-start.1 = (f32[72,144,144]{2,1,0:T(8,128)S(1)}, f32[72,144,144]{2,1,0:T(8,128)S(1)}, u32[]{:S(2)}, u32[]{:S(2)}) collective-permute-start(f32[72,144,144]{2,1,0:T(8,128)S(1)} %add.158), channel_id=1, source_target_pairs={{0,4},{2,6},{4,0},{6,2},{8,12},{10,14},{12,8},{14,10},{16,20},{18,... | collective-permute-start | bytes 17915912 | tf_op jit(solution)/shard_map/ppermute | solution.py:74
  422.1 229.7 %collective-permute-start.2 = (f32[72,144,144]{2,1,0:T(8,128)S(1)}, f32[72,144,144]{2,1,0:T(8,128)S(1)}, u32[]{:S(2)}, u32[]{:S(2)}) collective-permute-start(f32[72,144,144]{2,1,0:T(8,128)S(1)} %add.159), channel_id=1, source_target_pairs={{0,8},{2,10},{4,12},{6,14},{8,0},{10,2},{12,4},{14,6},{16,24},{18,... | collective-permute-start | bytes 17915912 | tf_op jit(solution)/shard_map/ppermute | solution.py:74
  656.7 457.5 %collective-permute-start.3 = (f32[72,144,144]{2,1,0:T(8,128)}, f32[72,144,144]{2,1,0:T(8,128)}, u32[]{:S(2)}, u32[]{:S(2)}) collective-permute-start(f32[72,144,144]{2,1,0:T(8,128)} %add.160), channel_id=1, source_target_pairs={{0,16},{2,18},{4,20},{6,22},{8,24},{10,26},{12,28},{14,30},{16,0},... | collective-permute-start | bytes 17915912 | tf_op jit(solution)/shard_map/ppermute | solution.py:74
  720.4 404.1 %copy-start.1 = (f32[288,144]{0,1:T(8,128)}, f32[288,144]{0,1:T(8,128)S(1)}, u32[]{:S(2)}) copy-start(f32[288,144]{0,1:T(8,128)S(1)} %fusion.3) | copy-start | bytes 497668
  1172.0 3.3 copy-start.2
